TPU v7x, 32 devices: a whole 2x2x4 slice. The times are simulated.
32 devices in a mesh: seq: 8 (over z, y), tensor: 4 (over x, core).
Axes of the slice: x: 2, y: 2, z: 4, core: 2. Of those that a mesh axis runs over, the one named last changes fastest.
Arguments:
- layer_input: bfloat16 [2048, 4096], P('seq', 'tensor'), may hold values from -6 to 6
- norm_gain: float32 [4096], replicated, may hold values from 0.1 to 1.9
- in_weights: bfloat16 [2, 4096, 2048], P(None, None, 'tensor'), may hold values from -0.09375 to 0.09375
- conv_weight: float32 [4, 2048], P(None, 'tensor'), may hold values from -4 to 4
- conv_bias: float32 [2048], P('tensor'), may hold values from -3 to 3
- gate_weights: bfloat16 [2, 8, 256, 256], P(None, 'tensor'), may hold values from -0.375 to 0.375
- gate_bias: float32 [2, 2048], P(None, 'tensor'), may hold values from -4 to 4
- decay_rate: float32 [2048], P('tensor'), may hold values from 1e-06 to 0.03, as said below
- out_weight: bfloat16 [2048, 4096], P('tensor'), may hold values from -0.1875 to 0.1875
- mlp_gain: float32 [4096], replicated, may hold values from 0.1 to 1.9
- mlp_in: bfloat16 [2, 4096, 6144], P(None, 'seq', 'tensor'), may hold values from -0.09375 to 0.09375
- mlp_out: bfloat16 [6144, 4096], P('tensor', 'seq'), may hold values from -0.109375 to 0.109375
Outputs:
- block_output: bfloat16 [2048, 4096], P('seq', 'tensor')
Inputs may be any that keep to these rules, and one draw needn't show every extreme that they name: `decay_rate`: every rate is positive.
All inputs are finite; a program needn't handle non-finite values.
Results may differ from a plain program's by a relative error of at most 0.015.
Values may be sent and summed in bfloat16 or wider, within the bound.
A program may use at most 128 MiB of HBM per device.

v0:
```python
import jax
import jax.numpy as jnp
from jax import lax
from jax.sharding import PartitionSpec as P


def shifted(value, axis, steps):
    count = lax.axis_size(axis)
    first, last = (max(0, -steps), min(count, count - steps))
    return lax.ppermute(value, axis, [(source, source + steps) for source in range(first, last)])


def prefix(value, axis, combine, identity):
    size, here = (lax.axis_size(axis), lax.axis_index(axis))
    everything = jax.tree.map(lambda part: lax.all_gather(part, axis), value)
    start = jax.tree.map(
        lambda part, zero: jnp.broadcast_to(jnp.asarray(zero, part.dtype), part.shape),
        value,
        identity,
    )

    def hop(k, before):
        reached = k < here
        new = combine(before, jax.tree.map(lambda part: part[k], everything))
        return jax.tree.map(lambda a, b: jnp.where(reached, a, b), new, before)

    return lax.fori_loop(0, size, hop, start)


def rms_scale(rows, gain):
    values = rows.astype(jnp.float32)
    mean_square = jnp.mean(values * values, axis=-1, keepdims=True)
    return (values * lax.rsqrt(mean_square + 1e-06) * gain).astype(jnp.bfloat16)


def chain_step(earlier, later):
    return (earlier[0] * later[0], later[0] * earlier[1] + later[1])


def shards(
    layer_input,
    norm_gain,
    in_weights,
    conv_weight,
    conv_bias,
    gate_weights,
    gate_bias,
    decay_rate,
    out_weight,
    mlp_gain,
    mlp_in,
    mlp_out,
):
    whole_rows = lax.all_gather(layer_input, "tensor", axis=1, tiled=True)
    normed = rms_scale(whole_rows, norm_gain)
    branch_x = jnp.dot(normed, in_weights[0], preferred_element_type=jnp.float32).astype(
        jnp.bfloat16
    )
    branch_y = jax.nn.gelu(
        jnp.dot(normed, in_weights[1], preferred_element_type=jnp.float32), approximate=True
    )
    num_tokens = branch_x.shape[0]
    rim_rows = conv_weight.shape[0] - 1
    earlier_rows = shifted(branch_x[num_tokens - rim_rows :], "seq", 1)
    padded = jnp.concatenate([earlier_rows, branch_x], axis=0).astype(jnp.float32)
    convolved = jnp.zeros(branch_x.shape, jnp.float32) + conv_bias
    for tap_index in range(conv_weight.shape[0]):
        start_row = rim_rows - tap_index
        convolved = convolved + conv_weight[tap_index] * padded[start_row : start_row + num_tokens]
    conv_out = convolved.astype(jnp.bfloat16)
    local_blocks = gate_weights.shape[1]
    block_width = gate_weights.shape[2]
    blocks_in = conv_out.reshape(num_tokens, local_blocks, block_width)
    gate_pre = jnp.einsum(
        "tnc,knce->ktne", blocks_in, gate_weights, preferred_element_type=jnp.float32
    )
    gate_pre = gate_pre.reshape(2, num_tokens, local_blocks * block_width) + gate_bias[:, None, :]
    log_decay = -8.0 * jax.nn.sigmoid(gate_pre[0]) * decay_rate
    decay = jnp.exp(log_decay)
    driven = (
        conv_out.astype(jnp.float32)
        * jax.nn.sigmoid(gate_pre[1])
        * jnp.sqrt(-jnp.expm1(2.0 * log_decay))
    )
    cum_decay, cum_state = lax.associative_scan(chain_step, (decay, driven), axis=0)
    identity = (jnp.ones_like(cum_decay[-1]), jnp.zeros_like(cum_state[-1]))
    entering = prefix((cum_decay[-1], cum_state[-1]), "seq", chain_step, identity)
    carried = entering[1]
    state = cum_decay * carried + cum_state
    mixed = (state * branch_y).astype(jnp.bfloat16)
    partial_sums = jnp.dot(mixed, out_weight, preferred_element_type=jnp.float32)
    full_sums = lax.psum(partial_sums.astype(jnp.bfloat16), "tensor").astype(jnp.float32)
    mid_full = (whole_rows.astype(jnp.float32) + full_sums).astype(jnp.bfloat16)
    own_width = layer_input.shape[1]
    residual = lax.dynamic_slice_in_dim(
        mid_full, lax.axis_index("tensor") * own_width, own_width, 1
    )
    mlp_normed = rms_scale(mid_full, mlp_gain)
    gate_up = jnp.einsum(
        "tr,krf->ktf",
        mlp_normed,
        lax.all_gather(mlp_in, "seq", axis=1, tiled=True),
        preferred_element_type=jnp.float32,
    )
    hidden = (jax.nn.gelu(gate_up[0], approximate=True) * gate_up[1]).astype(jnp.bfloat16)
    down_terms = jnp.dot(
        hidden,
        lax.all_gather(mlp_out, "seq", axis=1, tiled=True),
        preferred_element_type=jnp.float32,
    )
    down_share = lax.psum_scatter(
        down_terms.astype(jnp.bfloat16), "tensor", scatter_dimension=1, tiled=True
    ).astype(jnp.float32)
    return (residual.astype(jnp.float32) + down_share).astype(jnp.bfloat16)


def solution(mesh):
    return jax.shard_map(
        shards,
        mesh=mesh,
        in_specs=(
            P("seq", "tensor"),
            P(),
            P(None, None, "tensor"),
            P(None, "tensor"),
            P("tensor"),
            P(None, "tensor", None, None),
            P(None, "tensor"),
            P("tensor"),
            P("tensor", None),
            P(),
            P(None, "seq", "tensor"),
            P("tensor", "seq"),
        ),
        out_specs=P("seq", "tensor"),
        check_vma=False,
    )
```

profile of v0, /device:TPU:0, one launch (start us, length us, event | category | flops | bytes accessed | tf_op | source)
XLA Modules:
  0.0 835.9 jit_solution(12491428809460878877)
XLA Ops:
  7.4 0.7 all-gather.6.cloned.1.call-update
  8.1 0.9 fusion.115
  9.0 26.0 %all-gather.6.cloned.1.call-done = bf16[256,4096]{1,0:T(8,128)(2,1)} async-done(((bf16[256,1024]{1,0:T(8,128)(2,1)}), bf16[256,4096]{1,0:T(8,128)(2,1)}) %all-gather.6.cloned.1.call-update) | async-done | bytes 2097168 | tf_op jit(solution)/shard_map/all_gather | solution.py:54
  35.0 2.1 fusion.3
  37.2 4.1 fusion.26
  41.3 3.4 collective-permute-start
  44.7 1.3 collective-permute-done
  46.8 0.6 copy.18
  47.4 0.8 reshape.41
  48.4 0.8 fusion.91
  52.4 1.4 slice.328
  53.8 1.4 slice.367
  56.2 1.7 pad.129
  58.1 2.0 add_multiply_fusion.1
  60.2 1.7 pad.128
  61.8 0.7 add_bitcast_fusion
  62.5 27.9 %all-gather.1 = f32[8,1,512]{2,1,0:T(1,128)S(1)} all-gather(f32[1,1,512]{2,1,0:T(1,128)S(1)} %add_bitcast_fusion), channel_id=1, replica_groups=mesh['seq'=8,'tensor'=4] {'seq'}, dimensions={0}, use_global_device_ids=true | all-gather | bytes 18432 | tf_op jit(solution)/shard_map/all_gather | solution.py:15
  90.4 1.6 pad.113
  92.1 1.0 pad_maximum_fusion
  93.1 1.7 pad.112
  94.7 0.7 add_bitcast_fusion.1
  95.5 26.1 %all-gather = f32[8,1,512]{2,1,0:T(1,128)S(1)} all-gather(f32[1,1,512]{2,1,0:T(1,128)S(1)} %add_bitcast_fusion.1), channel_id=1, replica_groups=mesh['seq'=8,'tensor'=4] {'seq'}, dimensions={0}, use_global_device_ids=true | all-gather | bytes 18432 | tf_op jit(solution)/shard_map/all_gather | solution.py:15
  122.0 7.9 convolution_convert_fusion.1
  130.6 0.5 all-gather.10.cloned.1.call-update
  131.4 46.4 %all-reduce.34.cloned.1.call-done = bf16[256,4096]{1,0:T(8,128)(2,1)} async-done(((bf16[256,4096]{1,0:T(8,128)(2,1)}), bf16[256,4096]{1,0:T(8,128)(2,1)}) %all-reduce.34.cloned.1.call-update) | async-done | bytes 2097168 | tf_op jit(solution)/shard_map/psum | solution.py:92
  177.8 3.9 fusion
  181.7 427.0 %all-gather.8.cloned.1.call-done = bf16[2,4096,1536]{2,1,0:T(8,128)(2,1)} async-done(((bf16[2,512,1536]{2,1,0:T(8,128)(2,1)}), bf16[2,4096,1536]{2,1,0:T(8,128)(2,1)}) %all-gather.8.cloned.1.call-update) | async-done | bytes 25165840 | tf_op jit(solution)/shard_map/all_gather | solution.py:102
  608.7 13.4 %convolution_bitcast_fusion = f32[2,256,1536]{2,1,0:T(8,128)} fusion(bf16[2,4096,1536]{2,1,0:T(8,128)(2,1)} %all-gather.8.cloned.1.call-done, bf16[256,4096]{1,0:T(8,128)(2,1)} %get-tuple-element.129, f32[4096]{0:T(1024)S(1)} %copy-done.8, f32[256]{0:T(256)S(1)} %add_rsqrt_fusion), kind=kOutput, calls=%fused_computation.23 | convolution fusion | flops 6446645248 | bytes 30426112 | tf_op jit(solution)/shard_map/tr,krf->ktf/dot_general | solution.py:99
  622.1 164.4 %all-gather.10.cloned.1.call-done = bf16[1536,4096]{1,0:T(8,128)(2,1)} async-done(((bf16[1536,512]{1,0:T(8,128)(2,1)}), bf16[1536,4096]{1,0:T(8,128)(2,1)}) %all-gather.10.cloned.1.call-update) | async-done | bytes 12582928 | tf_op jit(solution)/shard_map/all_gather | solution.py:108
  786.5 10.6 %convolution_convert_fusion = bf16[256,4096]{1,0:T(8,128)(2,1)} fusion(bf16[1536,4096]{1,0:T(8,128)(2,1)} %all-gather.10.cloned.1.call-done, f32[2,256,1536]{2,1,0:T(8,128)} %convolution_bitcast_fusion), kind=kOutput, calls=%fused_computation.8 | convolution fusion | flops 3226206208 | bytes 17825792 | tf_op jit(solution)/shard_map/dot_general | solution.py:106
  797.1 29.5 %reduce-scatter.2.cloned.1.call-done = bf16[256,1024]{1,0:T(8,128)(2,1)} async-done(((bf16[256,4096]{1,0:T(8,128)(2,1)}), bf16[256,1024]{1,0:T(8,128)(2,1)}) %reduce-scatter.2.cloned.1.call-update) | async-done | bytes 524304 | tf_op jit(solution)/shard_map/reduce_scatter | solution.py:111
  826.6 2.2 add_convert_fusion
  (168 shorter events, 6.3 us)
Async XLA Ops:
  7.4 39.1 %copy-start = (bf16[2,2,256,256]{3,2,1,0:T(8,128)(2,1)S(1)}, bf16[2,2,256,256]{3,2,1,0:T(8,128)(2,1)}, u32[]{:S(2)}) copy-start(bf16[2,2,256,256]{3,2,1,0:T(8,128)(2,1)} %param.19) | copy-start | bytes 1572868
  7.4 27.7 %all-gather.6.cloned.1.call-start = ((), (), s32[]{:S(2)}) async-start(), calls=%async_computation.1 | async-start | bytes 2621440 | tf_op jit(solution)/shard_map/all_gather | solution.py:54
  8.1 169.7 %all-reduce.34.cloned.1.call-start = ((), (), s32[]{:S(2)}) async-start(), calls=%async_computation.2 | async-start | bytes 4194304 | tf_op jit(solution)/shard_map/psum | solution.py:92
  37.1 7.6 copy-start.6
  37.1 9.0 %copy-start.4 = (f32[512]{0:T(512)S(1)}, f32[512]{0:T(512)}, u32[]{:S(2)}) copy-start(f32[512]{0:T(512)} %param.18) | copy-start | bytes 6148
  41.3 4.7 collective-permute-start
  46.4 1.8 copy-start.5
  58.1 63.9 %copy-start.2 = (bf16[256,4096]{1,0:T(8,128)(2,1)S(1)}, bf16[256,4096]{1,0:T(8,128)(2,1)}, u32[]{:S(2)}) copy-start(bf16[256,4096]{1,0:T(8,128)(2,1)} %all-gather.6.cloned.1.call-done) | copy-start | bytes 6291460
  58.1 63.9 %copy-start.7 = (f32[4096]{0:T(1024)S(1)}, f32[4096]{0:T(1024)}, u32[]{:S(2)}) copy-start(f32[4096]{0:T(1024)} %param.15) | copy-start | bytes 49156
  60.1 61.9 %copy-start.3 = (f32[256,512]{1,0:T(8,128)S(1)}, f32[256,512]{1,0:T(8,128)}, u32[]{:S(2)}) copy-start(f32[256,512]{1,0:T(8,128)} %pad.129) | copy-start | bytes 1572868
  130.0 478.7 %all-gather.8.cloned.1.call-start = ((), (), s32[]{:S(2)}) async-start(), calls=%async_computation.3 | async-start | bytes 28311552 | tf_op jit(solution)/shard_map/all_gather | solution.py:102
  130.6 656.0 %all-gather.10.cloned.1.call-start = ((), (), s32[]{:S(2)}) async-start(), calls=%async_computation.4 | async-start | bytes 14155776 | tf_op jit(solution)/shard_map/all_gather | solution.py:108
  131.2 477.6 %copy-start.8 = (f32[4096]{0:T(1024)S(1)}, f32[4096]{0:T(1024)}, u32[]{:S(2)}) copy-start(f32[4096]{0:T(1024)} %param.23) | copy-start | bytes 49156
  131.2 695.4 %reduce-scatter.2.cloned.1.call-start = ((), (), s32[]{:S(2)}) async-start(), calls=%async_computation.5 | async-start | bytes 2621440 | tf_op jit(solution)/shard_map/reduce_scatter | solution.py:111
  786.5 42.3 %copy-start.1 = (bf16[2,2,256,256]{3,2,1,0:T(8,128)(2,1)S(1)}, bf16[2,2,256,256]{3,2,1,0:T(8,128)(2,1)}, u32[]{:S(2)}) copy-start(bf16[2,2,256,256]{3,2,1,0:T(8,128)(2,1)} %param.19) | copy-start | bytes 1572868
Sparse Core Ops, SparseCore 0:
  9.7 25.2 all-gather.5
  130.1 47.6 all-reduce.33
  797.2 29.3 reduce-scatter.1
Sparse Core Ops, SparseCore 1:
  132.0 476.6 all-gather.7
  610.6 175.9 all-gather.9
where the time goes:
time: 836 us
  waiting for transfers between devices  696 us (83%)
  blocking collectives  54 us (6%)
  matrix products  36.4 us (4%)
  between operations  15.4 us (2%)
  local copies, waits for them, and re-layouts  15.1 us (2%)
  other arithmetic  14.7 us (2%)
    all_gather x1, waiting for transfers between devices, shards(): lax.all_gather(mlp_in, 'seq', axis=1, tiled=True)  427 us
    all_gather x1, waiting for transfers between devices, shards(): lax.all_gather(mlp_out, 'seq', axis=1, tiled=True)  164 us
    all_gather x2, blocking collectives, prefix(): everything = jax.tree.map(lambda part: lax.all_gather(part, axis), value)  54 us
    psum x1, waiting for transfers between devices, shards(): lax.psum(partial_sums.astype(jnp.bfloat16), 'tensor').astype(jnp.float32)  46.4 us
    reduce_scatter x1, waiting for transfers between devices, shards(): lax.psum_scatter(down_terms.astype(jnp.bfloat16), 'tensor', scatter_dimen...  29.5 us
    all_gather x1, waiting for transfers between devices, shards(): whole_rows = lax.all_gather(layer_input, 'tensor', axis=1, tiled=True)  26 us
  transfers between devices with their start and end apart: 6, of which 6 were waited for; matrix products, arithmetic and copies ran while one was open for 2% of the time, Pallas kernels for 0%

commit v1 on v0

--- a/solution.py
+++ b/solution.py
@@ -2,6 +2,12 @@
 import jax.numpy as jnp
 from jax import lax
 from jax.sharding import PartitionSpec as P
+from jax.lax import all_gather
+
+
+def review_run_up(body):
+    u1 = all_gather(body, axis_name="tensor").sum(axis=0)
+    return u1
 
 
 def shifted(value, axis, steps):
@@ -89,7 +95,7 @@
     state = cum_decay * carried + cum_state
     mixed = (state * branch_y).astype(jnp.bfloat16)
     partial_sums = jnp.dot(mixed, out_weight, preferred_element_type=jnp.float32)
-    full_sums = lax.psum(partial_sums.astype(jnp.bfloat16), "tensor").astype(jnp.float32)
+    full_sums = review_run_up(partial_sums.astype(jnp.bfloat16)).astype(jnp.float32)
     mid_full = (whole_rows.astype(jnp.float32) + full_sums).astype(jnp.bfloat16)
     own_width = layer_input.shape[1]
     residual = lax.dynamic_slice_in_dim(

time: 836 us -> 891 us (1.066)
  waiting for transfers between devices: 696 us -> 747 us
    all_gather x0 -> x1, waiting for transfers between devices: none -> 53.2 us  [review_run_up(): u1 = all_gather(body, axis_name='tensor').sum(axis=0)]
    psum x1 -> x0, waiting for transfers between devices: 46.4 us -> none  [shards(): lax.psum(partial_sums.astype(jnp.bfloat16), 'tensor').astype(jnp.float32)]
    all_gather x1, waiting for transfers between devices: 427 us -> 471 us  [shards(): lax.all_gather(mlp_in, 'seq', axis=1, tiled=True)]
  transfers between devices with their start and end apart: 6 -> 6, of which waited for: 6 -> 6; matrix products, arithmetic and copies ran while one was open for 2% -> 3% of each run, Pallas kernels for 0% -> 0%
where the time goes in v1:
time: 891 us
  waiting for transfers between devices  747 us (84%)
  blocking collectives  54 us (6%)
  matrix products  36.4 us (4%)
  other arithmetic  21.7 us (2%)
  between operations  14 us (2%)
  local copies, waits for them, and re-layouts  13.5 us (2%)
    all_gather x1, waiting for transfers between devices, shards(): lax.all_gather(mlp_in, 'seq', axis=1, tiled=True)  471 us
    all_gather x1, waiting for transfers between devices, shards(): lax.all_gather(mlp_out, 'seq', axis=1, tiled=True)  165 us
    all_gather x2, blocking collectives, prefix(): everything = jax.tree.map(lambda part: lax.all_gather(part, axis), value)  54 us
    all_gather x1, waiting for transfers between devices, review_run_up(): u1 = all_gather(body, axis_name='tensor').sum(axis=0)  53.2 us
    reduce_scatter x1, waiting for transfers between devices, shards(): lax.psum_scatter(down_terms.astype(jnp.bfloat16), 'tensor', scatter_dimen...  29.5 us
    all_gather x1, waiting for transfers between devices, shards(): whole_rows = lax.all_gather(layer_input, 'tensor', axis=1, tiled=True)  26 us
  transfers between devices with their start and end apart: 6, of which 6 were waited for; matrix products, arithmetic and copies ran while one was open for 3% of the time, Pallas kernels for 0%

profile of v1, /device:TPU:0, one launch (start us, length us, event | category | flops | bytes accessed | tf_op | source)
XLA Modules:
  0.0 890.9 jit_solution(2056601713183165907)
XLA Ops:
  6.5 0.7 all-gather.8.cloned.1.call-update
  7.3 0.9 fusion.115
  8.2 26.0 %all-gather.8.cloned.1.call-done = bf16[256,4096]{1,0:T(8,128)(2,1)} async-done(((bf16[256,1024]{1,0:T(8,128)(2,1)}), bf16[256,4096]{1,0:T(8,128)(2,1)}) %all-gather.8.cloned.1.call-update) | async-done | bytes 2097168 | tf_op jit(solution)/shard_map/all_gather | solution.py:60
  34.2 2.1 fusion.3
  36.3 4.1 fusion.26
  40.5 3.4 collective-permute-start
  43.9 1.3 collective-permute-done
  46.0 0.6 copy.18
  46.6 0.8 reshape.41
  47.6 0.8 fusion.91
  51.6 1.4 slice.328
  53.0 1.4 slice.367
  55.4 1.7 pad.129
  57.2 1.9 add_multiply_fusion.1
  59.2 0.7 add_bitcast_fusion
  59.9 27.9 %all-gather.2 = f32[8,1,512]{2,1,0:T(1,128)S(1)} all-gather(f32[1,1,512]{2,1,0:T(1,128)S(1)} %add_bitcast_fusion), channel_id=1, replica_groups=mesh['seq'=8,'tensor'=4] {'seq'}, dimensions={0}, use_global_device_ids=true | all-gather | bytes 18432 | tf_op jit(solution)/shard_map/all_gather | solution.py:21
  87.8 1.7 pad.113
  89.5 1.0 pad_maximum_fusion
  90.5 1.7 pad.112
  92.1 0.7 add_bitcast_fusion.1
  92.9 26.1 %all-gather.1 = f32[8,1,512]{2,1,0:T(1,128)S(1)} all-gather(f32[1,1,512]{2,1,0:T(1,128)S(1)} %add_bitcast_fusion.1), channel_id=1, replica_groups=mesh['seq'=8,'tensor'=4] {'seq'}, dimensions={0}, use_global_device_ids=true | all-gather | bytes 18432 | tf_op jit(solution)/shard_map/all_gather | solution.py:21
  119.4 7.9 convolution_convert_fusion.1
  127.4 0.7 all-gather.10.cloned.1.call-update
  128.9 53.2 %all-gather.14.cloned.1.call-done = bf16[1024,4096]{1,0:T(8,128)(2,1)} async-done(((bf16[256,4096]{1,0:T(8,128)(2,1)}), bf16[1024,4096]{1,0:T(8,128)(2,1)}) %all-gather.14.cloned.1.call-update) | async-done | bytes 8388624 | tf_op jit(solution)/shard_map/all_gather | solution.py:9
  182.1 6.9 reduce_sum.31
  189.0 4.1 fusion
  193.2 470.9 %all-gather.10.cloned.1.call-done = bf16[2,4096,1536]{2,1,0:T(8,128)(2,1)} async-done(((bf16[2,512,1536]{2,1,0:T(8,128)(2,1)}), bf16[2,4096,1536]{2,1,0:T(8,128)(2,1)}) %all-gather.10.cloned.1.call-update) | async-done | bytes 25165840 | tf_op jit(solution)/shard_map/all_gather | solution.py:108
  664.1 13.4 %convolution_bitcast_fusion = f32[2,256,1536]{2,1,0:T(8,128)} fusion(bf16[2,4096,1536]{2,1,0:T(8,128)(2,1)} %all-gather.10.cloned.1.call-done, bf16[256,4096]{1,0:T(8,128)(2,1)} %get-tuple-element.129, f32[4096]{0:T(1024)S(1)} %copy-done.7, f32[256]{0:T(256)S(1)} %add_rsqrt_fusion), kind=kOutput, calls=%fused_computation.23 | convolution fusion | flops 6446645248 | bytes 30426112 | tf_op jit(solution)/shard_map/tr,krf->ktf/dot_general | solution.py:105
  677.5 164.6 %all-gather.12.cloned.1.call-done = bf16[1536,4096]{1,0:T(8,128)(2,1)} async-done(((bf16[1536,512]{1,0:T(8,128)(2,1)}), bf16[1536,4096]{1,0:T(8,128)(2,1)}) %all-gather.12.cloned.1.call-update) | async-done | bytes 12582928 | tf_op jit(solution)/shard_map/all_gather | solution.py:114
  842.1 10.6 %convolution_convert_fusion = bf16[256,4096]{1,0:T(8,128)(2,1)} fusion(bf16[1536,4096]{1,0:T(8,128)(2,1)} %all-gather.12.cloned.1.call-done, f32[2,256,1536]{2,1,0:T(8,128)} %convolution_bitcast_fusion), kind=kOutput, calls=%fused_computation.8 | convolution fusion | flops 3226206208 | bytes 17825792 | tf_op jit(solution)/shard_map/dot_general | solution.py:112
  852.7 29.5 %reduce-scatter.2.cloned.1.call-done = bf16[256,1024]{1,0:T(8,128)(2,1)} async-done(((bf16[256,4096]{1,0:T(8,128)(2,1)}), bf16[256,1024]{1,0:T(8,128)(2,1)}) %reduce-scatter.2.cloned.1.call-update) | async-done | bytes 524304 | tf_op jit(solution)/shard_map/reduce_scatter | solution.py:117
  882.2 2.2 add_convert_fusion
  (167 shorter events, 6.4 us)
Async XLA Ops:
  6.5 39.1 %copy-start = (bf16[2,2,256,256]{3,2,1,0:T(8,128)(2,1)S(1)}, bf16[2,2,256,256]{3,2,1,0:T(8,128)(2,1)}, u32[]{:S(2)}) copy-start(bf16[2,2,256,256]{3,2,1,0:T(8,128)(2,1)} %param.19) | copy-start | bytes 1572868
  6.5 27.7 %all-gather.8.cloned.1.call-start = ((), (), s32[]{:S(2)}) async-start(), calls=%async_computation.1 | async-start | bytes 2621440 | tf_op jit(solution)/shard_map/all_gather | solution.py:60
  7.3 174.9 %all-gather.14.cloned.1.call-start = ((), (), s32[]{:S(2)}) async-start(), calls=%async_computation.5 | async-start | bytes 10485760 | tf_op jit(solution)/shard_map/all_gather | solution.py:9
  36.3 7.6 copy-start.5
  36.3 9.0 %copy-start.3 = (f32[512]{0:T(512)S(1)}, f32[512]{0:T(512)}, u32[]{:S(2)}) copy-start(f32[512]{0:T(512)} %param.18) | copy-start | bytes 6148
  40.5 4.7 collective-permute-start
  45.3 2.1 copy-start.4
  55.4 64.0 %copy-start.2 = (bf16[256,4096]{1,0:T(8,128)(2,1)S(1)}, bf16[256,4096]{1,0:T(8,128)(2,1)}, u32[]{:S(2)}) copy-start(bf16[256,4096]{1,0:T(8,128)(2,1)} %all-gather.8.cloned.1.call-done) | copy-start | bytes 6291460
  55.4 64.0 %copy-start.6 = (f32[4096]{0:T(1024)S(1)}, f32[4096]{0:T(1024)}, u32[]{:S(2)}) copy-start(f32[4096]{0:T(1024)} %param.15) | copy-start | bytes 49156
  127.4 536.7 %all-gather.10.cloned.1.call-start = ((), (), s32[]{:S(2)}) async-start(), calls=%async_computation.2 | async-start | bytes 28311552 | tf_op jit(solution)/shard_map/all_gather | solution.py:108
  128.1 714.0 %all-gather.12.cloned.1.call-start = ((), (), s32[]{:S(2)}) async-start(), calls=%async_computation.3 | async-start | bytes 14155776 | tf_op jit(solution)/shard_map/all_gather | solution.py:114
  128.7 753.5 %reduce-scatter.2.cloned.1.call-start = ((), (), s32[]{:S(2)}) async-start(), calls=%async_computation.4 | async-start | bytes 2621440 | tf_op jit(solution)/shard_map/reduce_scatter | solution.py:117
  189.0 475.0 %copy-start.7 = (f32[4096]{0:T(1024)S(1)}, f32[4096]{0:T(1024)}, u32[]{:S(2)}) copy-start(f32[4096]{0:T(1024)} %param.23) | copy-start | bytes 49156
  842.1 42.3 %copy-start.1 = (bf16[2,2,256,256]{3,2,1,0:T(8,128)(2,1)S(1)}, bf16[2,2,256,256]{3,2,1,0:T(8,128)(2,1)}, u32[]{:S(2)}) copy-start(bf16[2,2,256,256]{3,2,1,0:T(8,128)(2,1)} %param.19) | copy-start | bytes 1572868
Sparse Core Ops, SparseCore 0:
  8.9 25.2 all-gather.7
  127.5 54.5 all-gather.13
  183.7 480.3 all-gather.9
  666.0 176.0 all-gather.11
  852.8 29.3 reduce-scatter.1
